TPU v7x, 64 devices: a 2x2x8 block of a 4x4x8 slice. The times are simulated.
64 devices in a mesh: dp: 4 (over x, y), tp: 16 (over z, core).
Axes of the slice: x: 2, y: 2, z: 8, core: 2. Of those that a mesh axis runs over, the one named last changes fastest.
The devices are a block of a 4x4x8 slice.
Arguments:
- k_cache: bfloat16 [64, 16, 1024, 128], P('dp', None, 'tp'), parts along dimension 0
- v_cache: bfloat16 [64, 16, 1024, 128], P('dp', None, 'tp'), parts along dimension 0
- prompt_len: int32 [64], P('dp'), parts along dimension 0
- x_steps: bfloat16 [64, 64, 2048], P(None, 'dp'), parts along dimension 1
- w_norm: bfloat16 [2048], replicated
- w_q: bfloat16 [2048, 2048], P(None, 'tp')
- w_k: bfloat16 [2048, 2048], P(None, 'tp')
- w_v: bfloat16 [2048, 2048], P(None, 'tp')
- w_o: bfloat16 [2048, 2048], P('tp')
Outputs:
- output 1: bfloat16 [64, 64, 2048], P(None, 'dp'), parts along dimension 1
- output 2: bfloat16 [64, 16, 1088, 128], P('dp', 'tp'), parts along dimension 0
- output 3: bfloat16 [64, 16, 1088, 128], P('dp', 'tp'), parts along dimension 0
There are 4 independent parts. A program takes and returns all parts, laid end to end along the dimension named above; an argument that names none is the same for every part.
All inputs are finite; a program needn't handle non-finite values.
Results may differ from a plain program's by a relative error of at most 0.0196691.
Values are sent between devices in bfloat16 or wider.
A program may use at most 768 MiB of HBM per device.

v0:
```python
import functools

import jax
import jax.numpy as jnp
from jax import lax
from jax.experimental import pallas as pl
from jax.experimental.pallas import tpu as pltpu
from jax.sharding import PartitionSpec as P

ROPE_BASE = 10000.0
NORM_EPS = 1e-6
CORES = 2
GROUP_ROWS = 2
PIECES = 4
X_STEPS = 8
MESH = pl.DeviceIdType.MESH
BF16 = jnp.bfloat16
F32 = jnp.float32


def main_kernel(n_tp, plen, freq, k_in, v_in, x_in, gain, w_q, w_k, w_v, w_o, k_buf, v_buf, y_buf,
                wq_v, wk_v, wv_v, x_blk, qkv, q_s, k_n, v_n, o_sr, o_snd, o_all, w_col, x_res,
                in_sem, x_sem, send_sem, recv_sem, w_send, w_recv, p_send, p_recv,
                o_send, o_recv, y_send, y_recv, d_send, d_recv):
    num_rows, out_len, head_dim = k_buf.shape
    n_steps, _, model_dim = x_in.shape
    slots = k_in.shape[2]
    seq_len = slots * n_tp
    chips = n_tp // CORES
    far = chips // 2
    half_steps = n_steps // CORES
    half_rows = half_steps * num_rows
    piece = half_rows // PIECES
    wide = CORES * head_dim
    n_groups = num_rows // GROUP_ROWS

    dp = lax.axis_index("dp")
    me = lax.axis_index("tp")
    chip = me // CORES
    core = lax.rem(me, CORES)
    other = 1 - core

    def chip_at(offset):
        return lax.rem(chip + offset + chips, chips)

    def device(chip_index, core_index):
        return (dp, chip_index * CORES + core_index)

    partner = device(chip, other)

    barrier = pltpu.get_barrier_semaphore()
    offsets = [0] + [s * d for d in range(1, far) for s in (1, -1)] + [far]
    for off in offsets:
        for c in range(CORES):
            if (off, c) != (0, 0):
                pl.semaphore_signal(barrier, inc=1, device_id=device(chip_at(off), lax.rem(core + c, CORES)), device_id_type=MESH)

    loads = [
        pltpu.make_async_copy(w_q, wq_v, in_sem.at[0]),
        pltpu.make_async_copy(w_k, wk_v, in_sem.at[1]),
        pltpu.make_async_copy(w_v, wv_v, in_sem.at[2]),
        pltpu.make_async_copy(
            x_in.at[pl.ds(core * half_steps, half_steps), :, pl.ds(pl.multiple_of(chip * wide, wide), wide)], x_res, in_sem.at[3]),
        pltpu.make_async_copy(
            w_o.at[:, pl.ds(pl.multiple_of(chip * wide, wide), wide)],
            w_col.at[chip, pl.ds(pl.multiple_of(core * head_dim, head_dim), head_dim)], in_sem.at[4]),
    ]
    for load in loads:
        load.start()

    def x_load(i, slot):
        return pltpu.make_async_copy(x_in.at[pl.ds(i * X_STEPS, X_STEPS)], x_blk.at[slot], x_sem.at[slot])

    x_load(0, 0).start()

    pl.semaphore_wait(barrier, n_tp - 1)

    my_slots = pl.ds(pl.multiple_of(me * slots, slots), slots)

    def send_group(i, _):
        rows = pl.ds(i * GROUP_ROWS, GROUP_ROWS)
        for which, (src, dst) in enumerate(((k_in, k_buf), (v_in, v_buf))):
            pltpu.make_async_copy(src.at[rows, me], dst.at[rows, my_slots], recv_sem.at[which, i]).start()
            for off in reversed(offsets):
                for c in range(CORES):
                    if (off, c) != (0, 0):
                        to_core = lax.rem(core + c, CORES)
                        to_chip = chip_at(off)
                        pltpu.make_async_remote_copy(
                            src_ref=src.at[rows, to_chip * CORES + to_core],
                            dst_ref=dst.at[rows, my_slots],
                            send_sem=send_sem.at[which, i],
                            recv_sem=recv_sem.at[which, i],
                            device_id=device(to_chip, to_core),
                            device_id_type=MESH,
                        ).start()
        return 0

    lax.fori_loop(0, n_groups, send_group, 0)

    w_copies = []
    for i, off in enumerate(reversed(offsets[1:])):
        to_chip = chip_at(off)
        w_copies.append(pltpu.make_async_remote_copy(
            src_ref=w_o.at[:, pl.ds(pl.multiple_of(to_chip * wide, wide), wide)],
            dst_ref=w_col.at[chip, pl.ds(pl.multiple_of(core * head_dim, head_dim), head_dim)],
            send_sem=w_send.at[i],
            recv_sem=w_recv.at[i],
            device_id=device(to_chip, core),
            device_id_type=MESH,
        ))
        w_copies[-1].start()

    for load in loads[:3]:
        load.wait()
    n_blocks = n_steps // X_STEPS
    blk_rows = X_STEPS * num_rows

    def project(i, _):
        slot = lax.rem(i, 2)

        @pl.when(i + 1 < n_blocks)
        def _():
            x_load(i + 1, 1 - slot).start()

        x_load(i, slot).wait()
        x = x_blk[slot].reshape(blk_rows, model_dim).astype(F32)
        inv = lax.rsqrt(jnp.mean(x * x, axis=-1, keepdims=True) + NORM_EPS)
        normed = (x * inv * (1.0 + gain[...].astype(F32))).astype(BF16)
        out = pl.ds(pl.multiple_of(i * blk_rows, blk_rows), blk_rows)
        for j, w in enumerate((wq_v, wk_v, wv_v)):
            qkv[j, out, :] = jnp.dot(normed, w[...], preferred_element_type=F32).astype(BF16).astype(F32)
        return 0

    lax.fori_loop(0, n_blocks, project, 0)

    def rope_row(b, _):
        step_id = lax.broadcasted_iota(jnp.int32, (n_steps, head_dim), 0)
        angle = (step_id + plen[b]).astype(F32) * freq[...]
        lane = lax.broadcasted_iota(jnp.int32, (n_steps, head_dim), 1)
        cos_part = jnp.cos(angle)
        sin_part = jnp.where(lane < head_dim // 2, -1.0, 1.0) * jnp.sin(angle)
        row = pl.ds(b, n_steps, stride=num_rows)

        def rotate(u):
            return u * cos_part + pltpu.roll(u, head_dim // 2, 1) * sin_part

        q_s[b] = (rotate(qkv[0, row, :]) * head_dim ** -0.5).astype(BF16)
        k_n[b] = rotate(qkv[1, row, :]).astype(BF16)
        v_n[b] = qkv[2, row, :].astype(BF16)
        for buf in (k_buf, v_buf):
            buf[b, seq_len:, :] = jnp.zeros((out_len - seq_len, head_dim), BF16)
        return 0

    lax.fori_loop(0, num_rows, rope_row, 0)

    def attend_row(b):
        start = plen[b]
        slot_id = lax.broadcasted_iota(jnp.int32, (out_len, n_steps), 0)
        step_id = lax.broadcasted_iota(jnp.int32, (out_len, n_steps), 1)
        pick = jnp.where(slot_id - step_id == start, 1.0, 0.0).astype(BF16)
        at = lax.broadcasted_iota(jnp.int32, (out_len, head_dim), 0) - start
        is_new = jnp.logical_and(at >= 0, at < n_steps)
        for buf, new in ((k_buf, k_n), (v_buf, v_n)):
            placed = jnp.dot(pick, new[b], preferred_element_type=F32)
            buf[b] = jnp.where(is_new, placed, buf[b].astype(F32)).astype(BF16)
        s = lax.dot_general(q_s[b], k_buf[b], (((1,), (1,)), ((), ())), preferred_element_type=F32)
        s_slot = lax.broadcasted_iota(jnp.int32, (n_steps, out_len), 1)
        s_step = lax.broadcasted_iota(jnp.int32, (n_steps, out_len), 0)
        s = jnp.where(s_slot - s_step <= start, s, -jnp.inf)
        e = jnp.exp(s - jnp.max(s, axis=-1, keepdims=True))
        a = (e / jnp.sum(e, axis=-1, keepdims=True)).astype(BF16)
        o = jnp.dot(a, v_buf[b], preferred_element_type=F32)
        o_sr[pl.ds(b, n_steps, stride=num_rows), :] = o.astype(BF16).astype(F32)

    def attend_group(i, _):
        rows = pl.ds(i * GROUP_ROWS, GROUP_ROWS)
        for which, buf in enumerate((k_buf, v_buf)):
            got = buf.at[rows, pl.ds(0, seq_len)]
            pltpu.make_async_copy(got, got, recv_sem.at[which, i]).wait()
        for r in range(GROUP_ROWS):
            attend_row(i * GROUP_ROWS + r)
        return 0

    lax.fori_loop(0, n_groups, attend_group, 0)

    my_lanes = pl.ds(pl.multiple_of(core * head_dim, head_dim), head_dim)
    mine = pl.ds(pl.multiple_of(core * half_rows, half_rows), half_rows)
    theirs = pl.ds(pl.multiple_of(other * half_rows, half_rows), half_rows)
    o_snd[...] = o_sr[theirs, :].astype(BF16)
    swap = pltpu.make_async_remote_copy(
        src_ref=o_snd, dst_ref=o_all.at[chip, :, my_lanes], send_sem=p_send.at[0], recv_sem=p_recv.at[0],
        device_id=partner, device_id_type=MESH)
    swap.start()
    o_all[chip, :, my_lanes] = o_sr[mine, :].astype(BF16)

    loads[3].wait()
    loads[4].wait()
    for copy in w_copies:
        copy.wait()
    w_swap = pltpu.make_async_remote_copy(
        src_ref=w_col.at[:, my_lanes], dst_ref=w_col.at[:, my_lanes], send_sem=p_send.at[1], recv_sem=p_recv.at[1],
        device_id=partner, device_id_type=MESH)
    w_swap.start()
    swap.wait()

    def hops(way, j):
        return far if (way + j) % 2 == 0 else far - 1

    def ring_copy(at, sems, way, hop, j):
        step = 1 if way == 0 else -1
        view = at(chip_at(-step * (hop - 1)), j)
        return pltpu.make_async_remote_copy(
            src_ref=view, dst_ref=view, send_sem=sems[0].at[way, hop - 1, j], recv_sem=sems[1].at[way, hop - 1, j],
            device_id=device(chip_at(step), core), device_id_type=MESH)

    def o_at(c, j):
        return o_all.at[c, pl.ds(j * piece, piece)]

    def y_at(c, j):
        return y_buf.at[pl.ds(pl.multiple_of(core * half_rows, half_rows) + j * piece, piece), pl.ds(pl.multiple_of(c * wide, wide), wide)]

    def hand_on(c, j):
        return pltpu.make_async_remote_copy(
            src_ref=y_at(c, j), dst_ref=y_at(c, j), send_sem=d_send.at[j], recv_sem=d_recv.at[j],
            device_id=partner, device_id_type=MESH)

    o_sems, y_sems = (o_send, o_recv), (y_send, y_recv)
    for j in range(PIECES):
        for way in range(2):
            ring_copy(o_at, o_sems, way, 1, j).start()

    def block_of_y(j):
        acc = x_res[j * (piece // num_rows):(j + 1) * (piece // num_rows)].reshape(piece, wide).astype(F32)
        total = jnp.zeros((piece, wide), F32)
        for c in range(chips):
            total += jnp.dot(o_all[c, j * piece:(j + 1) * piece, :], w_col[c], preferred_element_type=F32)
        y_buf[pl.ds(pl.multiple_of(core * half_rows, half_rows) + j * piece, piece), pl.ds(pl.multiple_of(chip * wide, wide), wide)] = (acc + total).astype(BF16)
        for way in range(2):
            ring_copy(y_at, y_sems, way, 1, j).start()
        hand_on(chip, j).start()

    for hop in range(1, far + 1):
        for j in range(PIECES):
            for way in range(2):
                if hop <= hops(way, j):
                    ring_copy(o_at, o_sems, way, hop, j).wait_recv()
                    if hop < hops(way, j):
                        ring_copy(o_at, o_sems, way, hop + 1, j).start()
            if hop == far:
                if j == 0:
                    w_swap.wait()
                block_of_y(j)
    for hop in range(1, far + 1):
        for j in range(PIECES):
            for way in range(2):
                if hop <= hops(way, j):
                    ring_copy(y_at, y_sems, way, hop, j).wait_recv()
                    if hop < hops(way, j):
                        ring_copy(y_at, y_sems, way, hop + 1, j).start()
                    hand_on(chip_at(-hop if way == 0 else hop), j).start()

    for i in range(n_groups):
        rows = pl.ds(i * GROUP_ROWS, GROUP_ROWS)
        for which, buf in enumerate((k_buf, v_buf)):
            sent = buf.at[rows, pl.ds(0, seq_len - slots)]
            pltpu.make_async_copy(sent, sent, send_sem.at[which, i]).wait()
    for hop in range(1, far + 1):
        for j in range(PIECES):
            for way in range(2):
                if hop <= hops(way, j):
                    ring_copy(o_at, o_sems, way, hop, j).wait_send()
                    ring_copy(y_at, y_sems, way, hop, j).wait_send()
    for j in range(PIECES):
        sent = y_buf.at[pl.ds(pl.multiple_of(core * half_rows, half_rows) + j * piece, piece)]
        pltpu.make_async_copy(sent, sent, d_send.at[j]).wait()
        got = y_buf.at[pl.ds(pl.multiple_of(other * half_rows, half_rows) + j * piece, piece)]
        pltpu.make_async_copy(got, got, d_recv.at[j]).wait()


def write_kernel(k_buf, v_buf, y_buf, k_out, v_out, y_out, sem):
    copies = [
        pltpu.make_async_copy(k_buf, k_out, sem.at[0]),
        pltpu.make_async_copy(v_buf, v_out, sem.at[1]),
        pltpu.make_async_copy(y_buf, y_out, sem.at[2]),
    ]
    for copy in copies:
        copy.start()
    for copy in copies:
        copy.wait()


def solution(mesh):
    n_tp = mesh.shape["tp"]

    def local_block(k_cache, v_cache, prompt_len, x_steps, w_norm, w_q, w_k, w_v, w_o):
        num_rows, _, slots, head_dim = k_cache.shape
        n_steps, _, model_dim = x_steps.shape
        out_len = slots * n_tp + n_steps
        chips = n_tp // CORES
        far = chips // 2
        half_rows = n_steps // CORES * num_rows
        wide = CORES * head_dim
        n_groups = num_rows // GROUP_ROWS
        lanes = jnp.arange(head_dim, dtype=jnp.int32) % (head_dim // 2)
        freq = (ROPE_BASE ** (-2.0 * lanes.astype(F32) / head_dim)).reshape(1, head_dim)
        dma = pltpu.SemaphoreType.DMA
        any_space = pl.BlockSpec(memory_space=pl.ANY)
        vmem = pl.BlockSpec(memory_space=pltpu.VMEM)
        cache = jax.ShapeDtypeStruct((num_rows, out_len, head_dim), BF16)
        k_buf, v_buf, y_buf = pl.pallas_call(
            functools.partial(main_kernel, n_tp),
            out_shape=(cache, cache, jax.ShapeDtypeStruct((n_steps * num_rows, model_dim), BF16)),
            in_specs=[pl.BlockSpec(memory_space=pltpu.SMEM), vmem, any_space, any_space, any_space, vmem] + [any_space] * 4,
            out_specs=(vmem, vmem, vmem),
            scratch_shapes=[
                pltpu.VMEM((model_dim, head_dim), BF16),
                pltpu.VMEM((model_dim, head_dim), BF16),
                pltpu.VMEM((model_dim, head_dim), BF16),
                pltpu.VMEM((2, X_STEPS, num_rows, model_dim), BF16),
                pltpu.VMEM((3, n_steps * num_rows, head_dim), F32),
                pltpu.VMEM((num_rows, n_steps, head_dim), BF16),
                pltpu.VMEM((num_rows, n_steps, head_dim), BF16),
                pltpu.VMEM((num_rows, n_steps, head_dim), BF16),
                pltpu.VMEM((n_steps * num_rows, head_dim), F32),
                pltpu.VMEM((half_rows, head_dim), BF16),
                pltpu.VMEM((chips, half_rows, wide), BF16),
                pltpu.VMEM((chips, wide, wide), BF16),
                pltpu.VMEM((n_steps // CORES, num_rows, wide), BF16),
                dma((5,)), dma((2,)),
                dma((2, n_groups)), dma((2, n_groups)),
                dma((chips - 1,)), dma((chips - 1,)),
                dma((2,)), dma((2,)),
                dma((2, far, PIECES)), dma((2, far, PIECES)),
                dma((2, far, PIECES)), dma((2, far, PIECES)),
                dma((PIECES,)), dma((PIECES,)),
            ],
            compiler_params=pltpu.CompilerParams(collective_id=0, has_side_effects=True, vmem_limit_bytes=44 * 2**20),
            name="decode_block",
        )(prompt_len, freq, k_cache, v_cache, x_steps, w_norm.reshape(1, model_dim), w_q, w_k, w_v, w_o)
        k_out, v_out, y_out = pl.pallas_call(
            write_kernel,
            out_shape=(cache, cache, jax.ShapeDtypeStruct((n_steps * num_rows, model_dim), BF16)),
            in_specs=[vmem, vmem, vmem],
            out_specs=(any_space, any_space, any_space),
            scratch_shapes=[dma((3,))],
            name="write_out",
        )(k_buf, v_buf, y_buf)
        return y_out.reshape(n_steps, num_rows, model_dim), k_out[:, None], v_out[:, None]

    cache_spec = P("dp", None, "tp", None)
    col_spec = P(None, "tp")
    out_cache_spec = P("dp", "tp", None, None)
    return jax.shard_map(local_block, mesh=mesh, in_specs=(cache_spec, cache_spec, P("dp"), P(None, "dp", None), P(None), col_spec, col_spec, col_spec, P("tp", None)), out_specs=(P(None, "dp", None), out_cache_spec, out_cache_spec), check_vma=False)
```

profile of v0, /device:TPU:21, one launch (start us, length us, event | category | flops | bytes accessed | tf_op | source)
XLA Modules:
  0.0 271.7 jit_solution(15581144248988366833)
XLA Ops:
  0.6 0.7 reshape.44.gain
  1.3 0.0 copy-start.1
  1.3 1.0 copy-done.1
  2.4 0.0 copy-start.2
  2.4 1.0 copy-done.2
  3.4 0.0 copy-start.3
  3.4 1.0 copy-done.3
  4.5 0.0 copy-start.4
  4.5 1.0 copy-done.4
  5.5 0.0 copy-start.5
  5.5 0.7 copy-done.5
  6.2 253.9 %decode_block.1 = (bf16[16,1088,128]{2,1,0:T(8,128)(2,1)}, bf16[16,1088,128]{2,1,0:T(8,128)(2,1)}, bf16[1024,2048]{1,0:T(8,128)(2,1)S(1)}) custom-call(s32[16]{0:T(128)S(1)} %copy-done.5, f32[1,128]{1,0:T(1,128)S(1)} %fusion.2.freq, bf16[16,16,64,128]{3,2,1,0:T(8,128)(2,1)} %k_in.1, bf16[16,16,64,128]{3,2,1,0:T(8,128)(2,1)} %v_in.1, ...), custom_call_target="tpu_custom_call" | custom-call | tf_op jit(solution)/shard_map/decode_block/pallas_call | solution.py:311
  260.0 0.0 copy-start
  260.0 2.0 copy-done
  262.0 9.7 %write_out.1 = (bf16[16,1088,128]{2,1,0:T(8,128)(2,1)}, bf16[16,1088,128]{2,1,0:T(8,128)(2,1)}, bf16[1024,2048]{1,0:T(8,128)(2,1)}) custom-call(bf16[16,1088,128]{2,1,0:T(8,128)(2,1)} %get-tuple-element.9.k_buf, bf16[16,1088,128]{2,1,0:T(8,128)(2,1)} %get-tuple-element.10.v_buf, bf16[1024,2048]{1,0:T(8,128)(2,1)} %copy-done), custom_call_target="tpu_custom_call" | custom-call | tf_op jit(solution)/shard_map/write_out/pallas_call | solution.py:341
  (1 shorter events, 0.0 us)
Async XLA Ops:
  1.3 1.0 copy-start.1
  2.4 1.0 copy-start.2
  3.4 1.0 copy-start.3
  4.5 1.0 copy-start.4
  5.5 0.7 copy-start.5
  260.0 2.0 copy-start
where the time goes:
time: 272 us
  Pallas kernels  264 us (97%)
  local copies, waits for them, and re-layouts  7.51 us (3%)
    pallas_call x1, Pallas kernels, local_block(): pl.pallas_call(functools.partial(main_kernel, n_tp), out_shape=(cache, ca...  254 us
    pallas_call x1, Pallas kernels, local_block(): pl.pallas_call(write_kernel, out_shape=(cache, cache, jax.ShapeDtypeStruc...  9.66 us
    unnamed x12, local copies, waits for them, and re-layouts  6.82 us

commit v1 on v0

v1 whole, which is shorter than its diff:
```python
import functools

import jax
import jax.numpy as jnp
from jax import lax
from jax.experimental import pallas as pl
from jax.experimental.pallas import tpu as pltpu
from jax.sharding import PartitionSpec as P

ROPE_BASE = 10000.0
NORM_EPS = 1e-6
CORES = 2
GROUP_ROWS = 2
BANDS = 2
CUTS = 2
X_STEPS = 8
MESH = pl.DeviceIdType.MESH
BF16 = jnp.bfloat16
F32 = jnp.float32


def main_kernel(n_tp, n_dp, plen_in, freq, gain, k_in, v_in, x_in, w_q, w_k, w_v, w_o, k_buf, v_buf, y_buf,
                plen, wq_v, wk_v, wv_v, x_blk, qkv, q_s, k_n, v_n, o_sr, o_snd, o_all, w_all, x_res,
                in_sem, x_sem, send_sem, recv_sem, w_send, w_recv, dp_send, dp_recv, p_send, p_recv,
                o_send, o_recv, d_send, d_recv):
    num_rows, out_len, head_dim = k_buf.shape
    n_steps, _, model_dim = x_in.shape
    slots = k_in.shape[2]
    seq_len = slots * n_tp
    chips = n_tp // CORES
    far = chips // 2
    half_steps = n_steps // CORES
    band = num_rows // BANDS
    band_rows = half_steps * band
    piece_steps = half_steps // CUTS
    piece = piece_steps * band
    wide = CORES * head_dim
    n_groups = num_rows // GROUP_ROWS
    share = model_dim // n_dp

    dp = lax.axis_index("dp")
    me = lax.axis_index("tp")
    chip = me // CORES
    core = lax.rem(me, CORES)
    other = 1 - core

    def chip_at(offset):
        return lax.rem(chip + offset + chips, chips)

    def device(chip_index, core_index):
        return (dp, chip_index * CORES + core_index)

    def sibling(offset):
        return (lax.rem(dp + offset, n_dp), me)

    partner = device(chip, other)
    offsets = [0] + [s * d for d in range(1, far) for s in (1, -1)] + [far]
    my_lanes = pl.ds(pl.multiple_of(core * head_dim, head_dim), head_dim)

    barrier = pltpu.get_barrier_semaphore()
    for off in offsets:
        for c in range(CORES):
            if (off, c) != (0, 0):
                pl.semaphore_signal(barrier, inc=1, device_id=device(chip_at(off), lax.rem(core + c, CORES)), device_id_type=MESH)
    for off in range(1, n_dp):
        pl.semaphore_signal(barrier, inc=1, device_id=sibling(off), device_id_type=MESH)

    my_share = pl.ds(pl.multiple_of(dp * share, share), share)
    loads = [
        pltpu.make_async_copy(plen_in, plen, in_sem.at[0]),
        pltpu.make_async_copy(w_q, wq_v, in_sem.at[1]),
        pltpu.make_async_copy(w_k, wk_v, in_sem.at[2]),
        pltpu.make_async_copy(w_v, wv_v, in_sem.at[3]),
        pltpu.make_async_copy(w_o.at[:, my_share], w_all.at[chip, my_lanes, my_share], in_sem.at[4]),
        pltpu.make_async_copy(x_in.at[pl.ds(core * half_steps, half_steps)], x_res, in_sem.at[5]),
    ]
    for load in loads:
        load.start()

    def x_load(i, slot):
        return pltpu.make_async_copy(x_in.at[pl.ds(i * X_STEPS, X_STEPS)], x_blk.at[slot], x_sem.at[slot])

    x_load(0, 0).start()

    with jax.named_scope("barrier"):
        pl.semaphore_wait(barrier, n_tp - 1 + n_dp - 1)

    def hops(way, j):
        return far if (way + j) % 2 == 0 else far - 1

    def ring_copy(at, sems, way, hop, j, first=None):
        step = 1 if way == 0 else -1
        view = at(chip_at(-step * (hop - 1)), j)
        return pltpu.make_async_remote_copy(
            src_ref=view if first is None else first, dst_ref=view,
            send_sem=sems[0].at[way, hop - 1, j], recv_sem=sems[1].at[way, hop - 1, j],
            device_id=device(chip_at(step), core), device_id_type=MESH)

    def ring_start(at, sems, hop, pieces):
        for j in pieces:
            for way in range(2):
                if hop <= hops(way, j):
                    ring_copy(at, sems, way, hop, j).start()

    def ring_turn(at, sems, hop, pieces):
        for j in pieces:
            for way in range(2):
                if hop <= hops(way, j):
                    ring_copy(at, sems, way, hop, j).wait_recv()
                    if hop < hops(way, j):
                        ring_copy(at, sems, way, hop + 1, j).start()

    def ring_drain(at, sems, pieces):
        for hop in range(1, far + 1):
            for j in pieces:
                for way in range(2):
                    if hop <= hops(way, j):
                        ring_copy(at, sems, way, hop, j).wait_send()

    w_half = head_dim // 2
    w_sems = (w_send, w_recv)

    def w_at(c, j):
        return w_all.at[c, pl.ds(pl.multiple_of(core * head_dim, head_dim) + j * w_half, w_half), my_share]

    for j in range(2):
        for way in range(2):
            ring_copy(w_at, w_sems, way, 1, j, w_o.at[pl.ds(j * w_half, w_half), my_share]).start()

    my_slots = pl.ds(pl.multiple_of(me * slots, slots), slots)

    def send_group(i, _):
        rows = pl.ds(i * GROUP_ROWS, GROUP_ROWS)
        for which, (src, dst) in enumerate(((k_in, k_buf), (v_in, v_buf))):
            pltpu.make_async_copy(src.at[rows, me], dst.at[rows, my_slots], recv_sem.at[which, i]).start()
            for off in reversed(offsets):
                for c in range(CORES):
                    if (off, c) != (0, 0):
                        to_core = lax.rem(core + c, CORES)
                        to_chip = chip_at(off)
                        pltpu.make_async_remote_copy(
                            src_ref=src.at[rows, to_chip * CORES + to_core],
                            dst_ref=dst.at[rows, my_slots],
                            send_sem=send_sem.at[which, i],
                            recv_sem=recv_sem.at[which, i],
                            device_id=device(to_chip, to_core),
                            device_id_type=MESH,
                        ).start()
        return 0

    send_group(0, 0)

    for load in loads[:4]:
        load.wait()
    n_blocks = n_steps // X_STEPS
    blk_rows = X_STEPS * num_rows

    def project(i, _):
        slot = lax.rem(i, 2)

        @pl.when(i + 1 < n_blocks)
        def _():
            x_load(i + 1, 1 - slot).start()

        x_load(i, slot).wait()
        x = x_blk[slot].reshape(blk_rows, model_dim).astype(F32)
        inv = lax.rsqrt(jnp.mean(x * x, axis=-1, keepdims=True) + NORM_EPS)
        normed = (x * inv * gain[...]).astype(BF16)
        out = pl.ds(pl.multiple_of(i * blk_rows, blk_rows), blk_rows)
        for j, w in enumerate((wq_v, wk_v, wv_v)):
            qkv[j, out, :] = jnp.dot(normed, w[...], preferred_element_type=F32).astype(BF16).astype(F32)
        return 0

    with jax.named_scope("project"):
        lax.fori_loop(0, n_blocks, project, 0)

    with jax.named_scope("w_hop1"):
        ring_turn(w_at, w_sems, 1, range(2))
    send_group(1, 0)

    def rope_row(b, _):
        step_id = lax.broadcasted_iota(jnp.int32, (n_steps, head_dim), 0)
        angle = (step_id + plen[b]).astype(F32) * freq[...]
        lane = lax.broadcasted_iota(jnp.int32, (n_steps, head_dim), 1)
        cos_part = jnp.cos(angle)
        sin_part = jnp.where(lane < head_dim // 2, -1.0, 1.0) * jnp.sin(angle)
        row = pl.ds(b, n_steps, stride=num_rows)

        def rotate(u):
            return u * cos_part + pltpu.roll(u, head_dim // 2, 1) * sin_part

        q_s[b] = (rotate(qkv[0, row, :]) * head_dim ** -0.5).astype(BF16)
        k_n[b] = rotate(qkv[1, row, :]).astype(BF16)
        v_n[b] = qkv[2, row, :].astype(BF16)
        for buf in (k_buf, v_buf):
            buf[b, seq_len:, :] = jnp.zeros((out_len - seq_len, head_dim), BF16)
        return 0

    with jax.named_scope("rope"):
        lax.fori_loop(0, num_rows, rope_row, 0)

    for hop in range(2, far):
        with jax.named_scope(f"w_hop{hop}"):
            ring_turn(w_at, w_sems, hop, range(2))
        send_group(hop, 0)
    with jax.named_scope(f"w_hop{far}"):
        ring_turn(w_at, w_sems, far, range(2))
    loads[4].wait()

    def to_sibling(off):
        view = w_all.at[:, my_lanes, my_share]
        return pltpu.make_async_remote_copy(
            src_ref=view, dst_ref=view, send_sem=dp_send.at[off - 1], recv_sem=dp_recv.at[off - 1],
            device_id=sibling(off), device_id_type=MESH)

    for off in range(1, n_dp):
        to_sibling(off).start()
    lax.fori_loop(far, n_groups, send_group, 0)

    w_swap = pltpu.make_async_remote_copy(
        src_ref=w_all.at[:, my_lanes], dst_ref=w_all.at[:, my_lanes], send_sem=p_send.at[BANDS], recv_sem=p_recv.at[BANDS],
        device_id=partner, device_id_type=MESH)

    def attend_row(b):
        start = plen[b]
        slot_id = lax.broadcasted_iota(jnp.int32, (out_len, n_steps), 0)
        step_id = lax.broadcasted_iota(jnp.int32, (out_len, n_steps), 1)
        pick = jnp.where(slot_id - step_id == start, 1.0, 0.0).astype(BF16)
        at = lax.broadcasted_iota(jnp.int32, (out_len, head_dim), 0) - start
        is_new = jnp.logical_and(at >= 0, at < n_steps)
        for buf, new in ((k_buf, k_n), (v_buf, v_n)):
            placed = jnp.dot(pick, new[b], preferred_element_type=F32)
            buf[b] = jnp.where(is_new, placed, buf[b].astype(F32)).astype(BF16)
        s = lax.dot_general(q_s[b], k_buf[b], (((1,), (1,)), ((), ())), preferred_element_type=F32)
        s_slot = lax.broadcasted_iota(jnp.int32, (n_steps, out_len), 1)
        s_step = lax.broadcasted_iota(jnp.int32, (n_steps, out_len), 0)
        s = jnp.where(s_slot - s_step <= start, s, -jnp.inf)
        e = jnp.exp(s - jnp.max(s, axis=-1, keepdims=True))
        a = (e / jnp.sum(e, axis=-1, keepdims=True)).astype(BF16)
        o = jnp.dot(a, v_buf[b], preferred_element_type=F32)
        o_sr[b // band, pl.ds(lax.rem(b, band), n_steps, stride=band), :] = o.astype(BF16).astype(F32)

    mine = pl.ds(pl.multiple_of(core * band_rows, band_rows), band_rows)
    theirs = pl.ds(pl.multiple_of(other * band_rows, band_rows), band_rows)
    o_sems = (o_send, o_recv)

    def swap(h):
        return pltpu.make_async_remote_copy(
            src_ref=o_snd.at[h], dst_ref=o_all.at[chip, pl.ds(h * band_rows, band_rows), my_lanes],
            send_sem=p_send.at[h], recv_sem=p_recv.at[h], device_id=partner, device_id_type=MESH)

    def swap_start(h):
        o_snd[h] = o_sr[h, theirs, :].astype(BF16)
        swap(h).start()
        o_all[chip, h * band_rows:(h + 1) * band_rows, my_lanes] = o_sr[h, mine, :].astype(BF16)

    def o_at(c, j):
        return o_all.at[c, pl.ds(j * piece, piece)]

    def band_pieces(h):
        return range(h * CUTS, (h + 1) * CUTS)

    def attend_group(i, _):
        rows = pl.ds(i * GROUP_ROWS, GROUP_ROWS)
        with jax.named_scope("wait_group"):
            for which, buf in enumerate((k_buf, v_buf)):
                got = buf.at[rows, pl.ds(0, seq_len)]
                pltpu.make_async_copy(got, got, recv_sem.at[which, i]).wait()
        with jax.named_scope("attend_group"):
            for r in range(GROUP_ROWS):
                attend_row(i * GROUP_ROWS + r)

        @pl.when(i == n_groups // 2 - 1)
        def _():
            swap_start(0)

        @pl.when(i == n_groups // 2)
        def _():
            swap(0).wait_recv()
            ring_start(o_at, o_sems, 1, band_pieces(0))

        @pl.when(i == n_groups - 3)
        def _():
            for off in range(1, n_dp):
                to_sibling(off).wait_recv()
            w_swap.start()

        return 0

    lax.fori_loop(0, n_groups, attend_group, 0)

    def y_at(of_core, j):
        first = pl.multiple_of(of_core * half_steps, half_steps) + (j % CUTS) * piece_steps
        return (pl.ds(first, piece_steps), pl.ds(j // CUTS * band, band))

    def hand_on(of_core, j):
        view = y_buf.at[y_at(of_core, j)]
        return pltpu.make_async_remote_copy(
            src_ref=view, dst_ref=view, send_sem=d_send.at[j], recv_sem=d_recv.at[j],
            device_id=partner, device_id_type=MESH)

    def y_piece(j):
        steps, rows = y_at(core, j)
        local = pl.ds((j % CUTS) * piece_steps, piece_steps)

        def columns(n, _):
            cols = pl.ds(pl.multiple_of(n * wide, wide), wide)
            total = jnp.dot(o_all[0, j * piece:(j + 1) * piece, :], w_all[0, :, cols], preferred_element_type=F32)
            for c in range(1, chips):
                total += jnp.dot(o_all[c, j * piece:(j + 1) * piece, :], w_all[c, :, cols], preferred_element_type=F32)
            x = x_res[local, rows, cols].astype(F32)
            y_buf[steps, rows, cols] = (x + total.reshape(piece_steps, band, wide)).astype(BF16)
            return 0

        with jax.named_scope("y_piece"):
            lax.fori_loop(0, model_dim // wide, columns, 0)
            hand_on(core, j).start()

    with jax.named_scope("swap1"):
        swap_start(1)
    with jax.named_scope("o_b0_hop1"):
        ring_turn(o_at, o_sems, 1, band_pieces(0))
    with jax.named_scope("o_b1_start"):
        swap(1).wait_recv()
        ring_start(o_at, o_sems, 1, band_pieces(1))
    loads[5].wait()
    w_swap.wait_recv()
    for hop in range(2, far + 1):
        with jax.named_scope(f"o_b0_hop{hop}"):
            ring_turn(o_at, o_sems, hop, band_pieces(0))
        with jax.named_scope(f"o_b1_hop{hop - 1}"):
            ring_turn(o_at, o_sems, hop - 1, band_pieces(1))
    for j in band_pieces(0):
        y_piece(j)
    for j in band_pieces(1):
        with jax.named_scope(f"o_b1_hop{far}"):
            ring_turn(o_at, o_sems, far, [j])
        y_piece(j)

    with jax.named_scope("drain"):
        for i in range(n_groups):
            rows = pl.ds(i * GROUP_ROWS, GROUP_ROWS)
            for which, buf in enumerate((k_buf, v_buf)):
                sent = buf.at[rows, pl.ds(0, seq_len - slots)]
                pltpu.make_async_copy(sent, sent, send_sem.at[which, i]).wait()
        ring_drain(w_at, w_sems, range(2))
        ring_drain(o_at, o_sems, range(BANDS * CUTS))
        for off in range(1, n_dp):
            to_sibling(off).wait_send()
        w_swap.wait_send()
        for h in range(BANDS):
            swap(h).wait_send()
        for j in range(BANDS * CUTS):
            hand_on(core, j).wait_send()
            hand_on(other, j).wait_recv()


def write_kernel(k_buf, v_buf, y_buf, k_out, v_out, y_out, sem):
    parts = sem.shape[1]
    copies = []
    for a, (src, dst) in enumerate(((k_buf, k_out), (v_buf, v_out), (y_buf, y_out))):
        size = src.shape[0] // parts
        for i in range(parts):
            copies.append(pltpu.make_async_copy(src.at[pl.ds(i * size, size)], dst.at[pl.ds(i * size, size)], sem.at[a, i]))
    for copy in copies:
        copy.start()
    for copy in copies:
        copy.wait()


def solution(mesh):
    n_tp = mesh.shape["tp"]
    n_dp = mesh.shape["dp"]

    def local_block(k_cache, v_cache, prompt_len, x_steps, w_norm, w_q, w_k, w_v, w_o):
        num_rows, _, slots, head_dim = k_cache.shape
        n_steps, _, model_dim = x_steps.shape
        out_len = slots * n_tp + n_steps
        chips = n_tp // CORES
        far = chips // 2
        half_steps = n_steps // CORES
        half_rows = half_steps * num_rows
        wide = CORES * head_dim
        n_groups = num_rows // GROUP_ROWS
        pieces = BANDS * CUTS
        lanes = jnp.arange(head_dim, dtype=jnp.int32) % (head_dim // 2)
        freq = (ROPE_BASE ** (-2.0 * lanes.astype(F32) / head_dim)).reshape(1, head_dim)
        gain = (1.0 + w_norm.astype(F32)).reshape(1, model_dim)
        dma = pltpu.SemaphoreType.DMA
        in_hbm = functools.partial(pltpu.with_memory_space_constraint, memory_space=pltpu.HBM)

        def in_vmem(shape):
            return pltpu.VMEM(shape.shape, shape.dtype)

        hbm = pl.BlockSpec(memory_space=pltpu.HBM)
        vmem = pl.BlockSpec(memory_space=pltpu.VMEM)
        cache = jax.ShapeDtypeStruct((num_rows, out_len, head_dim), BF16)
        y_shape = jax.ShapeDtypeStruct(x_steps.shape, BF16)
        k_buf, v_buf, y_buf = pl.pallas_call(
            functools.partial(main_kernel, n_tp, n_dp),
            out_shape=(in_vmem(cache), in_vmem(cache), in_vmem(y_shape)),
            in_specs=[hbm, vmem, vmem] + [hbm] * 7,
            out_specs=(vmem, vmem, vmem),
            scratch_shapes=[
                pltpu.SMEM(prompt_len.shape, jnp.int32),
                pltpu.VMEM((model_dim, head_dim), BF16),
                pltpu.VMEM((model_dim, head_dim), BF16),
                pltpu.VMEM((model_dim, head_dim), BF16),
                pltpu.VMEM((2, X_STEPS, num_rows, model_dim), BF16),
                pltpu.VMEM((3, n_steps * num_rows, head_dim), F32),
                pltpu.VMEM((num_rows, n_steps, head_dim), BF16),
                pltpu.VMEM((num_rows, n_steps, head_dim), BF16),
                pltpu.VMEM((num_rows, n_steps, head_dim), BF16),
                pltpu.VMEM((BANDS, n_steps * num_rows // BANDS, head_dim), F32),
                pltpu.VMEM((BANDS, half_rows // BANDS, head_dim), BF16),
                pltpu.VMEM((chips, half_rows, wide), BF16),
                pltpu.VMEM((chips, wide, model_dim), BF16),
                pltpu.VMEM((half_steps, num_rows, model_dim), BF16),
                dma((6,)), dma((2,)),
                dma((2, n_groups)), dma((2, n_groups)),
                dma((2, far, 2)), dma((2, far, 2)),
                dma((n_dp,)), dma((n_dp,)),
                dma((BANDS + 1,)), dma((BANDS + 1,)),
                dma((2, far, pieces)), dma((2, far, pieces)),
                dma((pieces,)), dma((pieces,)),
            ],
            compiler_params=pltpu.CompilerParams(collective_id=0, has_side_effects=True, vmem_limit_bytes=28 * 2**20),
            name="decode_block",
        )(in_hbm(prompt_len), freq, gain, *map(in_hbm, (k_cache, v_cache, x_steps, w_q, w_k, w_v, w_o)))
        k_out, v_out, y_out = pl.pallas_call(
            write_kernel,
            out_shape=(cache, cache, y_shape),
            in_specs=[vmem, vmem, vmem],
            out_specs=(hbm, hbm, hbm),
            scratch_shapes=[dma((3, 8))],
            compiler_params=pltpu.CompilerParams(vmem_limit_bytes=4 * 2**20),
            name="write_out",
        )(k_buf, v_buf, y_buf)
        return y_out, k_out[:, None], v_out[:, None]

    cache_spec = P("dp", None, "tp", None)
    col_spec = P(None, "tp")
    out_cache_spec = P("dp", "tp", None, None)
    return jax.shard_map(local_block, mesh=mesh, in_specs=(cache_spec, cache_spec, P("dp"), P(None, "dp", None), P(None), col_spec, col_spec, col_spec, P("tp", None)), out_specs=(P(None, "dp", None), out_cache_spec, out_cache_spec), check_vma=False)
```

time: 272 us -> 241 us (0.89)
  Pallas kernels: 264 us -> 239 us
  local copies, waits for them, and re-layouts: 7.51 us -> 0 us
    pallas_call x2, Pallas kernels: 264 us -> 239 us  [the longest x1 234 us: local_block(): pl.pallas_call(functools.partial(main_kernel, n_tp, n_dp), out_shape=(in_...]
    unnamed x12 -> x0, local copies, waits for them, and re-layouts: 6.82 us -> none
where the time goes in v1:
time: 241 us; the launch traced here: 240 us
  Pallas kernels  239 us (99%)
    pallas_call x1, Pallas kernels, local_block(): pl.pallas_call(functools.partial(main_kernel, n_tp, n_dp), out_shape=(in_...  234 us
    pallas_call x1, Pallas kernels, local_block(): pl.pallas_call(write_kernel, out_shape=(cache, cache, y_shape), in_specs=...  4.92 us

profile of v1, /device:TPU:21, one launch (start us, length us, event | category | flops | bytes accessed | tf_op | source)
XLA Modules:
  0.0 240.2 jit_solution(7988587121204945058)
XLA Ops:
  0.6 0.7 convert_add_fusion
  1.3 233.9 %decode_block.1 = (bf16[16,1088,128]{2,1,0:T(8,128)(2,1)S(1)}, bf16[16,1088,128]{2,1,0:T(8,128)(2,1)S(1)}, bf16[64,16,2048]{2,1,0:T(8,128)(2,1)S(1)}) custom-call(s32[16]{0:T(128)} %plen_in.1, f32[1,128]{1,0:T(1,128)S(1)} %fusion.2.freq, f32[1,2048]{1,0:T(1,128)S(1)} %bitcast.7, bf16[16,16,64,128]{3,2,1,0:T(8,128)(2,1)} %k_in.1, ...), custom_call_target="tpu_custom_call" | custom-call | tf_op jit(solution)/shard_map/decode_block/pallas_call | solution.py:399
  235.3 4.9 %write_out.1 = (bf16[16,1088,128]{2,1,0:T(8,128)(2,1)}, bf16[16,1088,128]{2,1,0:T(8,128)(2,1)}, bf16[64,16,2048]{2,1,0:T(8,128)(2,1)}) custom-call(bf16[16,1088,128]{2,1,0:T(8,128)(2,1)S(1)} %get-tuple-element.9.k_buf, bf16[16,1088,128]{2,1,0:T(8,128)(2,1)S(1)} %get-tuple-element.10.v_buf, bf16[64,16,2048]{2,1,0:T(8,128)(2,1)S(1)} %get-tuple-element.11.y_buf), custom_call_target="tpu_custom_call" | custom-call | tf_op jit(solution)/shard_map/write_out/pallas_call | solution.py:430
  (1 shorter events, 0.0 us)

commit v2 on v1

--- a/solution.py
+++ b/solution.py
@@ -20,7 +20,7 @@
 
 
 def main_kernel(n_tp, n_dp, plen_in, freq, gain, k_in, v_in, x_in, w_q, w_k, w_v, w_o, k_buf, v_buf, y_buf,
-                plen, wq_v, wk_v, wv_v, x_blk, qkv, q_s, k_n, v_n, o_sr, o_snd, o_all, w_all, x_res,
+                plen, wq_v, wk_v, wv_v, x_blk, qkv, q_s, k_n, v_n, o_sr, o_snd, o_all, w_all, x_res, y_acc,
                 in_sem, x_sem, send_sem, recv_sem, w_send, w_recv, dp_send, dp_recv, p_send, p_recv,
                 o_send, o_recv, d_send, d_recv):
     num_rows, out_len, head_dim = k_buf.shape
@@ -37,6 +37,7 @@
     wide = CORES * head_dim
     n_groups = num_rows // GROUP_ROWS
     share = model_dim // n_dp
+    quarter = y_acc.shape[1] // d_send.shape[1]
 
     dp = lax.axis_index("dp")
     me = lax.axis_index("tp")
@@ -289,53 +290,65 @@
 
     lax.fori_loop(0, n_groups, attend_group, 0)
 
-    def y_at(of_core, j):
-        first = pl.multiple_of(of_core * half_steps, half_steps) + (j % CUTS) * piece_steps
-        return (pl.ds(first, piece_steps), pl.ds(j // CUTS * band, band))
-
-    def hand_on(of_core, j):
-        view = y_buf.at[y_at(of_core, j)]
+    def y_view(of_core, h, cols):
+        return y_buf.at[pl.ds(pl.multiple_of(of_core * half_steps, half_steps), half_steps), pl.ds(h * band, band), cols]
+
+    def hand_on(of_core, h, q):
+        view = y_view(of_core, h, pl.ds(q * quarter, quarter))
         return pltpu.make_async_remote_copy(
-            src_ref=view, dst_ref=view, send_sem=d_send.at[j], recv_sem=d_recv.at[j],
+            src_ref=view, dst_ref=view, send_sem=d_send.at[h, q], recv_sem=d_recv.at[h, q],
             device_id=partner, device_id_type=MESH)
 
-    def y_piece(j):
-        steps, rows = y_at(core, j)
-        local = pl.ds((j % CUTS) * piece_steps, piece_steps)
-
-        def columns(n, _):
-            cols = pl.ds(pl.multiple_of(n * wide, wide), wide)
-            total = jnp.dot(o_all[0, j * piece:(j + 1) * piece, :], w_all[0, :, cols], preferred_element_type=F32)
-            for c in range(1, chips):
-                total += jnp.dot(o_all[c, j * piece:(j + 1) * piece, :], w_all[c, :, cols], preferred_element_type=F32)
-            x = x_res[local, rows, cols].astype(F32)
-            y_buf[steps, rows, cols] = (x + total.reshape(piece_steps, band, wide)).astype(BF16)
-            return 0
-
-        with jax.named_scope("y_piece"):
-            lax.fori_loop(0, model_dim // wide, columns, 0)
-            hand_on(core, j).start()
-
-    with jax.named_scope("swap1"):
-        swap_start(1)
-    with jax.named_scope("o_b0_hop1"):
-        ring_turn(o_at, o_sems, 1, band_pieces(0))
+    def y_add(h, froms, first=False, last=False):
+        rows = slice(h * band_rows, (h + 1) * band_rows)
+        for n in range(model_dim // wide):
+            cols = slice(n * wide, (n + 1) * wide)
+            total = None
+            for off in froms:
+                c = chip_at(off)
+                part = jnp.dot(o_all[c, rows, :], w_all[c, :, cols], preferred_element_type=F32)
+                total = part if total is None else total + part
+            if first:
+                total += x_res[:, h * band:(h + 1) * band, cols].astype(F32).reshape(band_rows, wide)
+            else:
+                total += y_acc[:, cols]
+            if last:
+                y_view(core, h, pl.ds(n * wide, wide))[...] = total.reshape(half_steps, band, wide).astype(BF16)
+                if (n + 1) * wide % quarter == 0:
+                    hand_on(core, h, n * wide // quarter).start()
+            else:
+                y_acc[:, cols] = total
+
+    def turn(h, hop):
+        with jax.named_scope(f"o_b{h}_hop{hop}"):
+            ring_turn(o_at, o_sems, hop, band_pieces(h))
+
+    def add(h, froms, **kwargs):
+        with jax.named_scope(f"y_b{h}"):
+            y_add(h, froms, **kwargs)
+
+    near = [s * d for d in range(1, far - 1) for s in (1, -1)]
+    edge = [far - 1, 1 - far]
+    swap_start(1)
+    turn(0, 1)
     with jax.named_scope("o_b1_start"):
         swap(1).wait_recv()
         ring_start(o_at, o_sems, 1, band_pieces(1))
     loads[5].wait()
     w_swap.wait_recv()
     for hop in range(2, far + 1):
-        with jax.named_scope(f"o_b0_hop{hop}"):
-            ring_turn(o_at, o_sems, hop, band_pieces(0))
-        with jax.named_scope(f"o_b1_hop{hop - 1}"):
-            ring_turn(o_at, o_sems, hop - 1, band_pieces(1))
-    for j in band_pieces(0):
-        y_piece(j)
-    for j in band_pieces(1):
-        with jax.named_scope(f"o_b1_hop{far}"):
-            ring_turn(o_at, o_sems, far, [j])
-        y_piece(j)
+        turn(0, hop)
+        if hop == far - 2:
+            add(0, [0] + near, first=True)
+        if hop == far - 1:
+            add(0, edge)
+        if hop == far:
+            add(0, [far], last=True)
+        turn(1, hop - 1)
+        if hop - 1 == far - 1:
+            add(1, [0] + near + edge, first=True)
+    turn(1, far)
+    add(1, [far], last=True)
 
     with jax.named_scope("drain"):
         for i in range(n_groups):
@@ -350,9 +363,10 @@
         w_swap.wait_send()
         for h in range(BANDS):
             swap(h).wait_send()
-        for j in range(BANDS * CUTS):
-            hand_on(core, j).wait_send()
-            hand_on(other, j).wait_recv()
+        for h in range(BANDS):
+            for q in range(model_dim // quarter):
+                hand_on(core, h, q).wait_send()
+                hand_on(other, h, q).wait_recv()
 
 
 def write_kernel(k_buf, v_buf, y_buf, k_out, v_out, y_out, sem):
@@ -416,13 +430,14 @@
                 pltpu.VMEM((chips, half_rows, wide), BF16),
                 pltpu.VMEM((chips, wide, model_dim), BF16),
                 pltpu.VMEM((half_steps, num_rows, model_dim), BF16),
+                pltpu.VMEM((half_rows // BANDS, model_dim), F32),
                 dma((6,)), dma((2,)),
                 dma((2, n_groups)), dma((2, n_groups)),
                 dma((2, far, 2)), dma((2, far, 2)),
                 dma((n_dp,)), dma((n_dp,)),
                 dma((BANDS + 1,)), dma((BANDS + 1,)),
                 dma((2, far, pieces)), dma((2, far, pieces)),
-                dma((pieces,)), dma((pieces,)),
+                dma((BANDS, 4)), dma((BANDS, 4)),
             ],
             compiler_params=pltpu.CompilerParams(collective_id=0, has_side_effects=True, vmem_limit_bytes=28 * 2**20),
             name="decode_block",

time: 241 us -> 235 us (0.975)
  Pallas kernels: 239 us -> 233 us
    pallas_call x1, Pallas kernels: 234 us -> 228 us  [local_block(): pl.pallas_call(functools.partial(main_kernel, n_tp, n_dp), out_shape=(in_...]
where the time goes in v2:
time: 235 us; the launch traced here: 234 us
  Pallas kernels  233 us (99%)
    pallas_call x1, Pallas kernels, local_block(): pl.pallas_call(functools.partial(main_kernel, n_tp, n_dp), out_shape=(in_...  228 us
    pallas_call x1, Pallas kernels, local_block(): pl.pallas_call(write_kernel, out_shape=(cache, cache, y_shape), in_specs=...  4.92 us

profile of v2, /device:TPU:21, one launch (start us, length us, event | category | flops | bytes accessed | tf_op | source)
XLA Modules:
  0.0 234.0 jit_solution(15524505007900934165)
XLA Ops:
  0.6 0.7 convert_add_fusion
  1.3 227.8 %decode_block.1 = (bf16[16,1088,128]{2,1,0:T(8,128)(2,1)S(1)}, bf16[16,1088,128]{2,1,0:T(8,128)(2,1)S(1)}, bf16[64,16,2048]{2,1,0:T(8,128)(2,1)S(1)}) custom-call(s32[16]{0:T(128)} %plen_in.1, f32[1,128]{1,0:T(1,128)S(1)} %fusion.2.freq, f32[1,2048]{1,0:T(1,128)S(1)} %bitcast.7, bf16[16,16,64,128]{3,2,1,0:T(8,128)(2,1)} %k_in.1, ...), custom_call_target="tpu_custom_call" | custom-call | tf_op jit(solution)/shard_map/decode_block/pallas_call | solution.py:413
  229.1 4.9 %write_out.1 = (bf16[16,1088,128]{2,1,0:T(8,128)(2,1)}, bf16[16,1088,128]{2,1,0:T(8,128)(2,1)}, bf16[64,16,2048]{2,1,0:T(8,128)(2,1)}) custom-call(bf16[16,1088,128]{2,1,0:T(8,128)(2,1)S(1)} %get-tuple-element.9.k_buf, bf16[16,1088,128]{2,1,0:T(8,128)(2,1)S(1)} %get-tuple-element.10.v_buf, bf16[64,16,2048]{2,1,0:T(8,128)(2,1)S(1)} %get-tuple-element.11.y_buf), custom_call_target="tpu_custom_call" | custom-call | tf_op jit(solution)/shard_map/write_out/pallas_call | solution.py:445
  (1 shorter events, 0.0 us)

commit v3 on v2

--- a/solution.py
+++ b/solution.py
@@ -19,8 +19,8 @@
 F32 = jnp.float32
 
 
-def main_kernel(n_tp, n_dp, plen_in, freq, gain, k_in, v_in, x_in, w_q, w_k, w_v, w_o, k_buf, v_buf, y_buf,
-                plen, wq_v, wk_v, wv_v, x_blk, qkv, q_s, k_n, v_n, o_sr, o_snd, o_all, w_all, x_res, y_acc,
+def main_kernel(n_tp, n_dp, plen_in, freq, w_norm, k_in, v_in, x_in, w_q, w_k, w_v, w_o, k_buf, v_buf, y_buf,
+                plen, norm_v, gain, wq_v, wk_v, wv_v, x_blk, qkv, q_s, k_n, v_n, o_sr, o_snd, o_all, w_all, x_res, y_acc,
                 in_sem, x_sem, send_sem, recv_sem, w_send, w_recv, dp_send, dp_recv, p_send, p_recv,
                 o_send, o_recv, d_send, d_recv):
     num_rows, out_len, head_dim = k_buf.shape
@@ -37,7 +37,7 @@
     wide = CORES * head_dim
     n_groups = num_rows // GROUP_ROWS
     share = model_dim // n_dp
-    quarter = y_acc.shape[1] // d_send.shape[1]
+    quarter = model_dim // 4
 
     dp = lax.axis_index("dp")
     me = lax.axis_index("tp")
@@ -74,6 +74,7 @@
         pltpu.make_async_copy(w_v, wv_v, in_sem.at[3]),
         pltpu.make_async_copy(w_o.at[:, my_share], w_all.at[chip, my_lanes, my_share], in_sem.at[4]),
         pltpu.make_async_copy(x_in.at[pl.ds(core * half_steps, half_steps)], x_res, in_sem.at[5]),
+        pltpu.make_async_copy(w_norm, norm_v, in_sem.at[6]),
     ]
     for load in loads:
         load.start()
@@ -94,29 +95,25 @@
         view = at(chip_at(-step * (hop - 1)), j)
         return pltpu.make_async_remote_copy(
             src_ref=view if first is None else first, dst_ref=view,
-            send_sem=sems[0].at[way, hop - 1, j], recv_sem=sems[1].at[way, hop - 1, j],
+            send_sem=sems[0], recv_sem=sems[1].at[way, hop - 1, j],
             device_id=device(chip_at(step), core), device_id_type=MESH)
 
+    def legs(hop, pieces):
+        by_way = [sorted(pieces, key=lambda j, way=way: -hops(way, j)) for way in range(2)]
+        return [(way, js[way]) for js in zip(*by_way) for way in range(2) if hop <= hops(way, js[way])]
+
     def ring_start(at, sems, hop, pieces):
-        for j in pieces:
-            for way in range(2):
-                if hop <= hops(way, j):
-                    ring_copy(at, sems, way, hop, j).start()
+        for way, j in legs(hop, pieces):
+            ring_copy(at, sems, way, hop, j).start()
 
     def ring_turn(at, sems, hop, pieces):
-        for j in pieces:
-            for way in range(2):
-                if hop <= hops(way, j):
-                    ring_copy(at, sems, way, hop, j).wait_recv()
-                    if hop < hops(way, j):
-                        ring_copy(at, sems, way, hop + 1, j).start()
-
-    def ring_drain(at, sems, pieces):
-        for hop in range(1, far + 1):
-            for j in pieces:
-                for way in range(2):
-                    if hop <= hops(way, j):
-                        ring_copy(at, sems, way, hop, j).wait_send()
+        for way, j in legs(hop, pieces):
+            ring_copy(at, sems, way, hop, j).wait_recv()
+            if hop < hops(way, j):
+                ring_copy(at, sems, way, hop + 1, j).start()
+
+    def wait_bytes(view, sem):
+        pltpu.make_async_copy(view, view, sem).wait()
 
     w_half = head_dim // 2
     w_sems = (w_send, w_recv)
@@ -124,9 +121,8 @@
     def w_at(c, j):
         return w_all.at[c, pl.ds(pl.multiple_of(core * head_dim, head_dim) + j * w_half, w_half), my_share]
 
-    for j in range(2):
-        for way in range(2):
-            ring_copy(w_at, w_sems, way, 1, j, w_o.at[pl.ds(j * w_half, w_half), my_share]).start()
+    for way, j in legs(1, range(2)):
+        ring_copy(w_at, w_sems, way, 1, j, w_o.at[pl.ds(j * w_half, w_half), my_share]).start()
 
     my_slots = pl.ds(pl.multiple_of(me * slots, slots), slots)
 
@@ -142,7 +138,7 @@
                         pltpu.make_async_remote_copy(
                             src_ref=src.at[rows, to_chip * CORES + to_core],
                             dst_ref=dst.at[rows, my_slots],
-                            send_sem=send_sem.at[which, i],
+                            send_sem=send_sem.at[which],
                             recv_sem=recv_sem.at[which, i],
                             device_id=device(to_chip, to_core),
                             device_id_type=MESH,
@@ -151,8 +147,9 @@
 
     send_group(0, 0)
 
-    for load in loads[:4]:
+    for load in (*loads[:4], loads[6]):
         load.wait()
+    gain[...] = 1.0 + norm_v[...].astype(F32).reshape(1, model_dim)
     n_blocks = n_steps // X_STEPS
     blk_rows = X_STEPS * num_rows
 
@@ -211,9 +208,10 @@
     def to_sibling(off):
         view = w_all.at[:, my_lanes, my_share]
         return pltpu.make_async_remote_copy(
-            src_ref=view, dst_ref=view, send_sem=dp_send.at[off - 1], recv_sem=dp_recv.at[off - 1],
+            src_ref=view, dst_ref=view, send_sem=dp_send, recv_sem=dp_recv,
             device_id=sibling(off), device_id_type=MESH)
 
+    others_share = w_all.at[:, pl.ds(0, head_dim), pl.ds(0, (n_dp - 1) * share)]
     for off in range(1, n_dp):
         to_sibling(off).start()
     lax.fori_loop(far, n_groups, send_group, 0)
@@ -265,8 +263,7 @@
         rows = pl.ds(i * GROUP_ROWS, GROUP_ROWS)
         with jax.named_scope("wait_group"):
             for which, buf in enumerate((k_buf, v_buf)):
-                got = buf.at[rows, pl.ds(0, seq_len)]
-                pltpu.make_async_copy(got, got, recv_sem.at[which, i]).wait()
+                wait_bytes(buf.at[rows, pl.ds(0, seq_len)], recv_sem.at[which, i])
         with jax.named_scope("attend_group"):
             for r in range(GROUP_ROWS):
                 attend_row(i * GROUP_ROWS + r)
@@ -282,8 +279,8 @@
 
         @pl.when(i == n_groups - 3)
         def _():
-            for off in range(1, n_dp):
-                to_sibling(off).wait_recv()
+            if n_dp > 1:
+                wait_bytes(others_share, dp_recv)
             w_swap.start()
 
         return 0
@@ -296,7 +293,7 @@
     def hand_on(of_core, h, q):
         view = y_view(of_core, h, pl.ds(q * quarter, quarter))
         return pltpu.make_async_remote_copy(
-            src_ref=view, dst_ref=view, send_sem=d_send.at[h, q], recv_sem=d_recv.at[h, q],
+            src_ref=view, dst_ref=view, send_sem=d_send.at[h], recv_sem=d_recv.at[h],
             device_id=partner, device_id_type=MESH)
 
     def y_add(h, froms, first=False, last=False):
@@ -351,22 +348,17 @@
     add(1, [far], last=True)
 
     with jax.named_scope("drain"):
-        for i in range(n_groups):
-            rows = pl.ds(i * GROUP_ROWS, GROUP_ROWS)
-            for which, buf in enumerate((k_buf, v_buf)):
-                sent = buf.at[rows, pl.ds(0, seq_len - slots)]
-                pltpu.make_async_copy(sent, sent, send_sem.at[which, i]).wait()
-        ring_drain(w_at, w_sems, range(2))
-        ring_drain(o_at, o_sems, range(BANDS * CUTS))
-        for off in range(1, n_dp):
-            to_sibling(off).wait_send()
+        for which, buf in enumerate((k_buf, v_buf)):
+            wait_bytes(buf.at[:, pl.ds(0, seq_len - slots)], send_sem.at[which])
+        wait_bytes(w_all.at[pl.ds(0, chips - 1), pl.ds(0, head_dim), pl.ds(0, share)], w_send)
+        wait_bytes(o_all.at[pl.ds(0, chips - 1)], o_send)
+        if n_dp > 1:
+            wait_bytes(others_share, dp_send)
         w_swap.wait_send()
         for h in range(BANDS):
             swap(h).wait_send()
-        for h in range(BANDS):
-            for q in range(model_dim // quarter):
-                hand_on(core, h, q).wait_send()
-                hand_on(other, h, q).wait_recv()
+            wait_bytes(y_view(core, h, pl.ds(0, model_dim)), d_send.at[h])
+            wait_bytes(y_view(other, h, pl.ds(0, model_dim)), d_recv.at[h])
 
 
 def write_kernel(k_buf, v_buf, y_buf, k_out, v_out, y_out, sem):
@@ -399,7 +391,6 @@
         pieces = BANDS * CUTS
         lanes = jnp.arange(head_dim, dtype=jnp.int32) % (head_dim // 2)
         freq = (ROPE_BASE ** (-2.0 * lanes.astype(F32) / head_dim)).reshape(1, head_dim)
-        gain = (1.0 + w_norm.astype(F32)).reshape(1, model_dim)
         dma = pltpu.SemaphoreType.DMA
         in_hbm = functools.partial(pltpu.with_memory_space_constraint, memory_space=pltpu.HBM)
 
@@ -413,10 +404,12 @@
         k_buf, v_buf, y_buf = pl.pallas_call(
             functools.partial(main_kernel, n_tp, n_dp),
             out_shape=(in_vmem(cache), in_vmem(cache), in_vmem(y_shape)),
-            in_specs=[hbm, vmem, vmem] + [hbm] * 7,
+            in_specs=[hbm, vmem] + [hbm] * 8,
             out_specs=(vmem, vmem, vmem),
             scratch_shapes=[
                 pltpu.SMEM(prompt_len.shape, jnp.int32),
+                pltpu.VMEM(w_norm.shape, BF16),
+                pltpu.VMEM((1, model_dim), F32),
                 pltpu.VMEM((model_dim, head_dim), BF16),
                 pltpu.VMEM((model_dim, head_dim), BF16),
                 pltpu.VMEM((model_dim, head_dim), BF16),
@@ -431,17 +424,17 @@
                 pltpu.VMEM((chips, wide, model_dim), BF16),
                 pltpu.VMEM((half_steps, num_rows, model_dim), BF16),
                 pltpu.VMEM((half_rows // BANDS, model_dim), F32),
-                dma((6,)), dma((2,)),
-                dma((2, n_groups)), dma((2, n_groups)),
-                dma((2, far, 2)), dma((2, far, 2)),
-                dma((n_dp,)), dma((n_dp,)),
+                dma((7,)), dma((2,)),
+                dma((2,)), dma((2, n_groups)),
+                dma, dma((2, far, 2)),
+                dma, dma,
                 dma((BANDS + 1,)), dma((BANDS + 1,)),
-                dma((2, far, pieces)), dma((2, far, pieces)),
-                dma((BANDS, 4)), dma((BANDS, 4)),
+                dma, dma((2, far, pieces)),
+                dma((BANDS,)), dma((BANDS,)),
             ],
             compiler_params=pltpu.CompilerParams(collective_id=0, has_side_effects=True, vmem_limit_bytes=28 * 2**20),
             name="decode_block",
-        )(in_hbm(prompt_len), freq, gain, *map(in_hbm, (k_cache, v_cache, x_steps, w_q, w_k, w_v, w_o)))
+        )(in_hbm(prompt_len), freq, *map(in_hbm, (w_norm, k_cache, v_cache, x_steps, w_q, w_k, w_v, w_o)))
         k_out, v_out, y_out = pl.pallas_call(
             write_kernel,
             out_shape=(cache, cache, y_shape),

time: 235 us -> 235 us (level)
  no operation moved by 1% of the time
where the time goes in v3:
time: 235 us; the launch traced here: 232 us
  Pallas kernels  231 us (98%)
    pallas_call x1, Pallas kernels, local_block(): pl.pallas_call(functools.partial(main_kernel, n_tp, n_dp), out_shape=(in_...  226 us
    pallas_call x1, Pallas kernels, local_block(): pl.pallas_call(write_kernel, out_shape=(cache, cache, y_shape), in_specs=...  4.92 us

profile of v3, /device:TPU:21, one launch (start us, length us, event | category | flops | bytes accessed | tf_op | source)
XLA Modules:
  0.0 232.0 jit_solution(5401446761428678355)
XLA Ops:
  0.6 226.4 %decode_block.1 = (bf16[16,1088,128]{2,1,0:T(8,128)(2,1)S(1)}, bf16[16,1088,128]{2,1,0:T(8,128)(2,1)S(1)}, bf16[64,16,2048]{2,1,0:T(8,128)(2,1)S(1)}) custom-call(s32[16]{0:T(128)} %plen_in.1, f32[1,128]{1,0:T(1,128)S(1)} %fusion.2.freq, bf16[2048]{0:T(1024)(128)(2,1)} %w_norm.1, bf16[16,16,64,128]{3,2,1,0:T(8,128)(2,1)} %k_in.1, ...), custom_call_target="tpu_custom_call" | custom-call | tf_op jit(solution)/shard_map/decode_block/pallas_call | solution.py:404
  227.1 4.9 %write_out.1 = (bf16[16,1088,128]{2,1,0:T(8,128)(2,1)}, bf16[16,1088,128]{2,1,0:T(8,128)(2,1)}, bf16[64,16,2048]{2,1,0:T(8,128)(2,1)}) custom-call(bf16[16,1088,128]{2,1,0:T(8,128)(2,1)S(1)} %get-tuple-element.9.k_buf, bf16[16,1088,128]{2,1,0:T(8,128)(2,1)S(1)} %get-tuple-element.10.v_buf, bf16[64,16,2048]{2,1,0:T(8,128)(2,1)S(1)} %get-tuple-element.11.y_buf), custom_call_target="tpu_custom_call" | custom-call | tf_op jit(solution)/shard_map/write_out/pallas_call | solution.py:438
  (1 shorter events, 0.0 us)

commit v4 on v3

--- a/solution.py
+++ b/solution.py
@@ -130,8 +130,8 @@
         rows = pl.ds(i * GROUP_ROWS, GROUP_ROWS)
         for which, (src, dst) in enumerate(((k_in, k_buf), (v_in, v_buf))):
             pltpu.make_async_copy(src.at[rows, me], dst.at[rows, my_slots], recv_sem.at[which, i]).start()
-            for off in reversed(offsets):
-                for c in range(CORES):
+            for c in range(CORES):
+                for off in reversed(offsets):
                     if (off, c) != (0, 0):
                         to_core = lax.rem(core + c, CORES)
                         to_chip = chip_at(off)

time: 235 us -> 233 us (level); the launches traced: 232 us -> 233 us
  no operation moved by 1% of the time
where the time goes in v4:
time: 233 us
  Pallas kernels  232 us (100%)
    pallas_call x1, Pallas kernels, local_block(): pl.pallas_call(functools.partial(main_kernel, n_tp, n_dp), out_shape=(in_...  227 us
    pallas_call x1, Pallas kernels, local_block(): pl.pallas_call(write_kernel, out_shape=(cache, cache, y_shape), in_specs=...  4.92 us

profile of v4, /device:TPU:21, one launch (start us, length us, event | category | flops | bytes accessed | tf_op | source)
XLA Modules:
  0.0 232.8 jit_solution(16329457350043179483)
XLA Ops:
  0.6 227.2 %decode_block.1 = (bf16[16,1088,128]{2,1,0:T(8,128)(2,1)S(1)}, bf16[16,1088,128]{2,1,0:T(8,128)(2,1)S(1)}, bf16[64,16,2048]{2,1,0:T(8,128)(2,1)S(1)}) custom-call(s32[16]{0:T(128)} %plen_in.1, f32[1,128]{1,0:T(1,128)S(1)} %fusion.2.freq, bf16[2048]{0:T(1024)(128)(2,1)} %w_norm.1, bf16[16,16,64,128]{3,2,1,0:T(8,128)(2,1)} %k_in.1, ...), custom_call_target="tpu_custom_call" | custom-call | tf_op jit(solution)/shard_map/decode_block/pallas_call | solution.py:404
  227.9 4.9 %write_out.1 = (bf16[16,1088,128]{2,1,0:T(8,128)(2,1)}, bf16[16,1088,128]{2,1,0:T(8,128)(2,1)}, bf16[64,16,2048]{2,1,0:T(8,128)(2,1)}) custom-call(bf16[16,1088,128]{2,1,0:T(8,128)(2,1)S(1)} %get-tuple-element.9.k_buf, bf16[16,1088,128]{2,1,0:T(8,128)(2,1)S(1)} %get-tuple-element.10.v_buf, bf16[64,16,2048]{2,1,0:T(8,128)(2,1)S(1)} %get-tuple-element.11.y_buf), custom_call_target="tpu_custom_call" | custom-call | tf_op jit(solution)/shard_map/write_out/pallas_call | solution.py:438
  (1 shorter events, 0.0 us)

commit v5 on v4

--- a/solution.py
+++ b/solution.py
@@ -102,10 +102,6 @@
         by_way = [sorted(pieces, key=lambda j, way=way: -hops(way, j)) for way in range(2)]
         return [(way, js[way]) for js in zip(*by_way) for way in range(2) if hop <= hops(way, js[way])]
 
-    def ring_start(at, sems, hop, pieces):
-        for way, j in legs(hop, pieces):
-            ring_copy(at, sems, way, hop, j).start()
-
     def ring_turn(at, sems, hop, pieces):
         for way, j in legs(hop, pieces):
             ring_copy(at, sems, way, hop, j).wait_recv()
@@ -259,6 +255,15 @@
     def band_pieces(h):
         return range(h * CUTS, (h + 1) * CUTS)
 
+    def o_start(h):
+        swap_start(h)
+        for way, j in legs(1, band_pieces(h)):
+            view = o_all.at[chip, pl.ds(j * piece, piece), my_lanes]
+            for to_core, src in ((core, view), (other, o_snd.at[h, pl.ds(j % CUTS * piece, piece)])):
+                pltpu.make_async_remote_copy(
+                    src_ref=src, dst_ref=view, send_sem=o_send, recv_sem=o_recv.at[way, 0, j],
+                    device_id=device(chip_at(1 if way == 0 else -1), to_core), device_id_type=MESH).start()
+
     def attend_group(i, _):
         rows = pl.ds(i * GROUP_ROWS, GROUP_ROWS)
         with jax.named_scope("wait_group"):
@@ -270,12 +275,7 @@
 
         @pl.when(i == n_groups // 2 - 1)
         def _():
-            swap_start(0)
-
-        @pl.when(i == n_groups // 2)
-        def _():
-            swap(0).wait_recv()
-            ring_start(o_at, o_sems, 1, band_pieces(0))
+            o_start(0)
 
         @pl.when(i == n_groups - 3)
         def _():
@@ -308,13 +308,13 @@
             if first:
                 total += x_res[:, h * band:(h + 1) * band, cols].astype(F32).reshape(band_rows, wide)
             else:
-                total += y_acc[:, cols]
+                total += y_acc[h, :, cols]
             if last:
                 y_view(core, h, pl.ds(n * wide, wide))[...] = total.reshape(half_steps, band, wide).astype(BF16)
                 if (n + 1) * wide % quarter == 0:
                     hand_on(core, h, n * wide // quarter).start()
             else:
-                y_acc[:, cols] = total
+                y_acc[h, :, cols] = total
 
     def turn(h, hop):
         with jax.named_scope(f"o_b{h}_hop{hop}"):
@@ -326,25 +326,25 @@
 
     near = [s * d for d in range(1, far - 1) for s in (1, -1)]
     edge = [far - 1, 1 - far]
-    swap_start(1)
+    o_start(1)
     turn(0, 1)
-    with jax.named_scope("o_b1_start"):
-        swap(1).wait_recv()
-        ring_start(o_at, o_sems, 1, band_pieces(1))
-    loads[5].wait()
-    w_swap.wait_recv()
+    turn(1, 1)
     for hop in range(2, far + 1):
         turn(0, hop)
         if hop == far - 2:
+            loads[5].wait()
+            w_swap.wait_recv()
+            for h in range(BANDS):
+                swap(h).wait_recv()
             add(0, [0] + near, first=True)
         if hop == far - 1:
             add(0, edge)
+            add(1, [0] + near, first=True)
         if hop == far:
             add(0, [far], last=True)
-        turn(1, hop - 1)
-        if hop - 1 == far - 1:
-            add(1, [0] + near + edge, first=True)
-    turn(1, far)
+        turn(1, hop)
+        if hop == far - 1:
+            add(1, edge)
     add(1, [far], last=True)
 
     with jax.named_scope("drain"):
@@ -423,7 +423,7 @@
                 pltpu.VMEM((chips, half_rows, wide), BF16),
                 pltpu.VMEM((chips, wide, model_dim), BF16),
                 pltpu.VMEM((half_steps, num_rows, model_dim), BF16),
-                pltpu.VMEM((half_rows // BANDS, model_dim), F32),
+                pltpu.VMEM((BANDS, half_rows // BANDS, model_dim), F32),
                 dma((7,)), dma((2,)),
                 dma((2,)), dma((2, n_groups)),
                 dma, dma((2, far, 2)),

time: 233 us -> 231 us (level)
  no operation moved by 1% of the time
where the time goes in v5:
time: 231 us
  Pallas kernels  231 us (100%)
    pallas_call x1, Pallas kernels, local_block(): pl.pallas_call(functools.partial(main_kernel, n_tp, n_dp), out_shape=(in_...  226 us
    pallas_call x1, Pallas kernels, local_block(): pl.pallas_call(write_kernel, out_shape=(cache, cache, y_shape), in_specs=...  4.92 us

profile of v5, /device:TPU:21, one launch (start us, length us, event | category | flops | bytes accessed | tf_op | source)
XLA Modules:
  0.0 231.2 jit_solution(12410197438992357991)
XLA Ops:
  0.6 225.7 %decode_block.1 = (bf16[16,1088,128]{2,1,0:T(8,128)(2,1)S(1)}, bf16[16,1088,128]{2,1,0:T(8,128)(2,1)S(1)}, bf16[64,16,2048]{2,1,0:T(8,128)(2,1)S(1)}) custom-call(s32[16]{0:T(128)} %plen_in.1, f32[1,128]{1,0:T(1,128)S(1)} %fusion.2.freq, bf16[2048]{0:T(1024)(128)(2,1)} %w_norm.1, bf16[16,16,64,128]{3,2,1,0:T(8,128)(2,1)} %k_in.1, ...), custom_call_target="tpu_custom_call" | custom-call | tf_op jit(solution)/shard_map/decode_block/pallas_call | solution.py:404
  226.3 4.9 %write_out.1 = (bf16[16,1088,128]{2,1,0:T(8,128)(2,1)}, bf16[16,1088,128]{2,1,0:T(8,128)(2,1)}, bf16[64,16,2048]{2,1,0:T(8,128)(2,1)}) custom-call(bf16[16,1088,128]{2,1,0:T(8,128)(2,1)S(1)} %get-tuple-element.9.k_buf, bf16[16,1088,128]{2,1,0:T(8,128)(2,1)S(1)} %get-tuple-element.10.v_buf, bf16[64,16,2048]{2,1,0:T(8,128)(2,1)S(1)} %get-tuple-element.11.y_buf), custom_call_target="tpu_custom_call" | custom-call | tf_op jit(solution)/shard_map/write_out/pallas_call | solution.py:438
  (1 shorter events, 0.0 us)

commit v6 on v5

--- a/solution.py
+++ b/solution.py
@@ -19,10 +19,10 @@
 F32 = jnp.float32
 
 
-def main_kernel(n_tp, n_dp, plen_in, freq, w_norm, k_in, v_in, x_in, w_q, w_k, w_v, w_o, k_buf, v_buf, y_buf,
-                plen, norm_v, gain, wq_v, wk_v, wv_v, x_blk, qkv, q_s, k_n, v_n, o_sr, o_snd, o_all, w_all, x_res, y_acc,
+def main_kernel(n_tp, n_dp, plen_in, freq, w_norm, k_in, v_in, x_in, w_q, w_k, w_v, w_o, k_buf, v_buf, y_buf, o_all, w_all, o_oth, y_acc,
+                plen, norm_v, gain, wq_v, wk_v, wv_v, x_blk, qkv, q_s, k_n, v_n, o_sr, o_snd, x_res, x_oth,
                 in_sem, x_sem, send_sem, recv_sem, w_send, w_recv, dp_send, dp_recv, p_send, p_recv,
-                o_send, o_recv, d_send, d_recv):
+                o_send, o_recv, d_send, d_recv, g_send, g_recv):
     num_rows, out_len, head_dim = k_buf.shape
     n_steps, _, model_dim = x_in.shape
     slots = k_in.shape[2]
@@ -75,6 +75,8 @@
         pltpu.make_async_copy(w_o.at[:, my_share], w_all.at[chip, my_lanes, my_share], in_sem.at[4]),
         pltpu.make_async_copy(x_in.at[pl.ds(core * half_steps, half_steps)], x_res, in_sem.at[5]),
         pltpu.make_async_copy(w_norm, norm_v, in_sem.at[6]),
+        pltpu.make_async_copy(
+            x_in.at[pl.ds(other * half_steps, half_steps), pl.ds((BANDS - 1) * band, band)], x_oth, in_sem.at[7]),
     ]
     for load in loads:
         load.start()
@@ -102,11 +104,13 @@
         by_way = [sorted(pieces, key=lambda j, way=way: -hops(way, j)) for way in range(2)]
         return [(way, js[way]) for js in zip(*by_way) for way in range(2) if hop <= hops(way, js[way])]
 
-    def ring_turn(at, sems, hop, pieces):
+    def ring_turn(at, sems, hop, pieces, then=None):
         for way, j in legs(hop, pieces):
             ring_copy(at, sems, way, hop, j).wait_recv()
             if hop < hops(way, j):
                 ring_copy(at, sems, way, hop + 1, j).start()
+            if then is not None:
+                then(chip_at(-hop if way == 0 else hop), j)
 
     def wait_bytes(view, sem):
         pltpu.make_async_copy(view, view, sem).wait()
@@ -297,35 +301,50 @@
             device_id=partner, device_id_type=MESH)
 
     def y_add(h, froms, first=False, last=False):
-        rows = slice(h * band_rows, (h + 1) * band_rows)
+        passed = h == BANDS
+        rows = slice(0, band_rows) if passed else slice(h * band_rows, (h + 1) * band_rows)
+        o_ref = o_oth if passed else o_all
         for n in range(model_dim // wide):
             cols = slice(n * wide, (n + 1) * wide)
             total = None
             for off in froms:
                 c = chip_at(off)
-                part = jnp.dot(o_all[c, rows, :], w_all[c, :, cols], preferred_element_type=F32)
+                part = jnp.dot(o_ref[c, rows, :], w_all[c, :, cols], preferred_element_type=F32)
                 total = part if total is None else total + part
             if first:
-                total += x_res[:, h * band:(h + 1) * band, cols].astype(F32).reshape(band_rows, wide)
+                x = x_oth[:, :, cols] if passed else x_res[:, h * band:(h + 1) * band, cols]
+                total += x.astype(F32).reshape(band_rows, wide)
             else:
                 total += y_acc[h, :, cols]
             if last:
-                y_view(core, h, pl.ds(n * wide, wide))[...] = total.reshape(half_steps, band, wide).astype(BF16)
-                if (n + 1) * wide % quarter == 0:
+                y_view(other if passed else core, min(h, BANDS - 1), pl.ds(n * wide, wide))[...] = total.reshape(half_steps, band, wide).astype(BF16)
+                if h < BANDS - 1 and (n + 1) * wide % quarter == 0:
                     hand_on(core, h, n * wide // quarter).start()
             else:
                 y_acc[h, :, cols] = total
 
+    def pass_on(stage):
+        def start(c, j):
+            pltpu.make_async_remote_copy(
+                src_ref=o_all.at[c, pl.ds(j * piece, piece)], dst_ref=o_oth.at[c, pl.ds(j % CUTS * piece, piece)],
+                send_sem=g_send, recv_sem=g_recv.at[stage], device_id=partner, device_id_type=MESH).start()
+        return start
+
+    near = [s * d for d in range(1, far - 1) for s in (1, -1)]
+    edge = [far - 1, 1 - far]
+
     def turn(h, hop):
         with jax.named_scope(f"o_b{h}_hop{hop}"):
-            ring_turn(o_at, o_sems, hop, band_pieces(h))
+            then = pass_on(max(0, hop - far + 2)) if h == BANDS - 1 else None
+            ring_turn(o_at, o_sems, hop, band_pieces(h), then)
 
     def add(h, froms, **kwargs):
         with jax.named_scope(f"y_b{h}"):
+            if h == BANDS:
+                stage = 0 if "first" in kwargs else 2 if "last" in kwargs else 1
+                wait_bytes(o_oth.at[pl.ds(0, len(froms))], g_recv.at[stage])
             y_add(h, froms, **kwargs)
 
-    near = [s * d for d in range(1, far - 1) for s in (1, -1)]
-    edge = [far - 1, 1 - far]
     o_start(1)
     turn(0, 1)
     turn(1, 1)
@@ -333,19 +352,25 @@
         turn(0, hop)
         if hop == far - 2:
             loads[5].wait()
+            loads[7].wait()
             w_swap.wait_recv()
             for h in range(BANDS):
                 swap(h).wait_recv()
+            for j in band_pieces(1):
+                pass_on(0)(chip, j)
             add(0, [0] + near, first=True)
         if hop == far - 1:
             add(0, edge)
-            add(1, [0] + near, first=True)
+            add(2, [0] + near, first=True)
         if hop == far:
             add(0, [far], last=True)
         turn(1, hop)
+        if hop == far - 2:
+            add(1, [0] + near, first=True)
         if hop == far - 1:
             add(1, edge)
-    add(1, [far], last=True)
+    for stage, count in ((1, 2), (2, 1)):
+        wait_bytes(o_oth.at[pl.ds(0, count)], g_recv.at[stage])
 
     with jax.named_scope("drain"):
         for which, buf in enumerate((k_buf, v_buf)):
@@ -357,19 +382,44 @@
         w_swap.wait_send()
         for h in range(BANDS):
             swap(h).wait_send()
+        for h in range(BANDS - 1):
             wait_bytes(y_view(core, h, pl.ds(0, model_dim)), d_send.at[h])
             wait_bytes(y_view(other, h, pl.ds(0, model_dim)), d_recv.at[h])
-
-
-def write_kernel(k_buf, v_buf, y_buf, k_out, v_out, y_out, sem):
+        wait_bytes(o_oth, g_send)
+
+
+def write_kernel(k_buf, v_buf, y_buf, o_all, w_all, o_oth, y_acc, k_out, v_out, y_out, y_last, sem, y_sem):
+    n_steps, num_rows, model_dim = y_buf.shape
+    chips, band_rows, wide = o_oth.shape
+    half_steps, band = n_steps // CORES, num_rows // BANDS
+    me = lax.axis_index("tp")
+    core = lax.rem(me, CORES)
+    far = chips // 2
+    late = [lax.rem(me // CORES + off + chips, chips) for off in (far, far - 1, 1 - far)]
     parts = sem.shape[1]
     copies = []
-    for a, (src, dst) in enumerate(((k_buf, k_out), (v_buf, v_out), (y_buf, y_out))):
+    for a, (src, dst) in enumerate(((k_buf, k_out), (v_buf, v_out))):
         size = src.shape[0] // parts
         for i in range(parts):
             copies.append(pltpu.make_async_copy(src.at[pl.ds(i * size, size)], dst.at[pl.ds(i * size, size)], sem.at[a, i]))
+    done = pl.ds(0, num_rows - band)
+    copies.append(pltpu.make_async_copy(y_buf.at[:, done], y_out.at[:, done], y_sem.at[CORES]))
     for copy in copies:
         copy.start()
+
+    rest = pl.ds(num_rows - band, band)
+    for half in range(CORES):
+        of_core = lax.rem(core + half, CORES)
+        steps = pl.ds(pl.multiple_of(of_core * half_steps, half_steps), half_steps)
+        for n in range(model_dim // wide):
+            cols = slice(n * wide, (n + 1) * wide)
+            total = y_acc[BANDS - 1 + half, :, cols]
+            for c in (late if half else late[:1]):
+                o = o_oth[c] if half else o_all[c, (BANDS - 1) * band_rows:, :]
+                total += jnp.dot(o, w_all[c, :, cols], preferred_element_type=F32)
+            y_last[half, :, :, cols] = total.reshape(half_steps, band, wide).astype(BF16)
+        copies.append(pltpu.make_async_copy(y_last.at[half], y_out.at[steps, rest], y_sem.at[half]))
+        copies[-1].start()
     for copy in copies:
         copy.wait()
 
@@ -401,11 +451,17 @@
         vmem = pl.BlockSpec(memory_space=pltpu.VMEM)
         cache = jax.ShapeDtypeStruct((num_rows, out_len, head_dim), BF16)
         y_shape = jax.ShapeDtypeStruct(x_steps.shape, BF16)
-        k_buf, v_buf, y_buf = pl.pallas_call(
+        rest = (
+            jax.ShapeDtypeStruct((chips, half_rows, wide), BF16),
+            jax.ShapeDtypeStruct((chips, wide, model_dim), BF16),
+            jax.ShapeDtypeStruct((chips, half_rows // BANDS, wide), BF16),
+            jax.ShapeDtypeStruct((BANDS + 1, half_rows // BANDS, model_dim), F32),
+        )
+        bufs = pl.pallas_call(
             functools.partial(main_kernel, n_tp, n_dp),
-            out_shape=(in_vmem(cache), in_vmem(cache), in_vmem(y_shape)),
+            out_shape=tuple(map(in_vmem, (cache, cache, y_shape, *rest))),
             in_specs=[hbm, vmem] + [hbm] * 8,
-            out_specs=(vmem, vmem, vmem),
+            out_specs=(vmem,) * 7,
             scratch_shapes=[
                 pltpu.SMEM(prompt_len.shape, jnp.int32),
                 pltpu.VMEM(w_norm.shape, BF16),
@@ -420,30 +476,29 @@
                 pltpu.VMEM((num_rows, n_steps, head_dim), BF16),
                 pltpu.VMEM((BANDS, n_steps * num_rows // BANDS, head_dim), F32),
                 pltpu.VMEM((BANDS, half_rows // BANDS, head_dim), BF16),
-                pltpu.VMEM((chips, half_rows, wide), BF16),
-                pltpu.VMEM((chips, wide, model_dim), BF16),
                 pltpu.VMEM((half_steps, num_rows, model_dim), BF16),
-                pltpu.VMEM((BANDS, half_rows // BANDS, model_dim), F32),
-                dma((7,)), dma((2,)),
+                pltpu.VMEM((half_steps, num_rows // BANDS, model_dim), BF16),
+                dma((8,)), dma((2,)),
                 dma((2,)), dma((2, n_groups)),
                 dma, dma((2, far, 2)),
                 dma, dma,
                 dma((BANDS + 1,)), dma((BANDS + 1,)),
                 dma, dma((2, far, pieces)),
                 dma((BANDS,)), dma((BANDS,)),
+                dma, dma((3,)),
             ],
-            compiler_params=pltpu.CompilerParams(collective_id=0, has_side_effects=True, vmem_limit_bytes=28 * 2**20),
+            compiler_params=pltpu.CompilerParams(collective_id=0, has_side_effects=True, vmem_limit_bytes=24 * 2**20),
             name="decode_block",
         )(in_hbm(prompt_len), freq, *map(in_hbm, (w_norm, k_cache, v_cache, x_steps, w_q, w_k, w_v, w_o)))
         k_out, v_out, y_out = pl.pallas_call(
             write_kernel,
             out_shape=(cache, cache, y_shape),
-            in_specs=[vmem, vmem, vmem],
+            in_specs=[vmem] * 7,
             out_specs=(hbm, hbm, hbm),
-            scratch_shapes=[dma((3, 8))],
-            compiler_params=pltpu.CompilerParams(vmem_limit_bytes=4 * 2**20),
+            scratch_shapes=[pltpu.VMEM((CORES, half_steps, num_rows // BANDS, model_dim), BF16), dma((2, 8)), dma((CORES + 1,))],
+            compiler_params=pltpu.CompilerParams(vmem_limit_bytes=8 * 2**20),
             name="write_out",
-        )(k_buf, v_buf, y_buf)
+        )(*bufs)
         return y_out, k_out[:, None], v_out[:, None]
 
     cache_spec = P("dp", None, "tp", None)

time: 231 us -> 230 us (level)
  no operation moved by 1% of the time
where the time goes in v6:
time: 230 us
  Pallas kernels  229 us (100%)
    pallas_call x1, Pallas kernels, local_block(): pl.pallas_call(functools.partial(main_kernel, n_tp, n_dp), out_shape=tupl...  224 us
    pallas_call x1, Pallas kernels, local_block(): pl.pallas_call(write_kernel, out_shape=(cache, cache, y_shape), in_specs=...  4.91 us

profile of v6, /device:TPU:21, one launch (start us, length us, event | category | flops | bytes accessed | tf_op | source)
XLA Modules:
  0.0 229.9 jit_solution(4146201699414831129)
XLA Ops:
  0.6 224.4 %decode_block.1 = (bf16[16,1088,128]{2,1,0:T(8,128)(2,1)S(1)}, bf16[16,1088,128]{2,1,0:T(8,128)(2,1)S(1)}, bf16[64,16,2048]{2,1,0:T(8,128)(2,1)S(1)}, bf16[8,512...) custom-call(s32[16]{0:T(128)} %plen_in.1, ...), custom_call_target="tpu_custom_call" | custom-call | tf_op jit(solution)/shard_map/decode_block/pallas_call | solution.py:460
  225.0 4.9 %write_out.1 = (bf16[16,1088,128]{2,1,0:T(8,128)(2,1)}, bf16[16,1088,128]{2,1,0:T(8,128)(2,1)}, bf16[64,16,2048]{2,1,0:T(8,128)(2,1)}) custom-call(bf16[16,1088,128]{2,1,0:T(8,128)(2,1)S(1)} %get-tuple-element.13.k_buf, bf16[16,1088,128]{2,1,0:T(8,128)(2,1)S(1)} %get-tuple-element.14.v_buf, bf16[64,16,2048]{2,1,0:T(8,128)(2,1)S(1)} %get-tuple-element.15.y_buf, ...), custom_call_target="tpu_custom_call" | custom-call | tf_op jit(solution)/shard_map/write_out/pallas_call | solution.py:493
  (1 shorter events, 0.0 us)
